TPU v7x, 32 devices: a whole 2x2x4 slice. The times are simulated.
32 devices in a mesh: dp: 8 (over z, core), seq: 4 (over y, x).
Axes of the slice: x: 2, y: 2, z: 4, core: 2. Of those that a mesh axis runs over, the one named last changes fastest.
Arguments:
- tokens: bfloat16 [32, 256, 1024], P(('dp', 'seq')), may hold values from -6 to 6
- queries: bfloat16 [32, 256, 1024], P(('dp', 'seq')), may hold values from -240 to 240
- keys: bfloat16 [32, 256, 1024], P(('dp', 'seq')), may hold values from -7 to 7
- values: bfloat16 [32, 256, 1024], P(('dp', 'seq')), may hold values from -6 to 6
- ln_gain: bfloat16 [1024], replicated, may hold values from 0.5 to 1.5
- mean_in: bfloat16 [1024, 2048], P(None, 'seq'), may hold values from -0.1875 to 0.1875
- sigma_in: bfloat16 [1024, 2048], P(None, 'seq'), may hold values from 0.0039978027 to 0.029907227
- noise_in: bfloat16 [1024, 2048], P(None, 'seq'), may hold values from -4 to 4
- mean_out: bfloat16 [2048, 1024], P('seq'), may hold values from -0.125 to 0.125
- sigma_out: bfloat16 [2048, 1024], P('seq'), may hold values from 0.0019989014 to 0.014953613
- noise_out: bfloat16 [2048, 1024], P('seq'), may hold values from -4 to 4
- flip_in: int32 [32, 1024], P('dp'), may hold values from -1 to 1, as said below
- flip_mid: int32 [32, 2048], P('dp', 'seq'), may hold values from -1 to 1, as said below
- flip_hidden: int32 [32, 2048], P('dp', 'seq'), may hold values from -1 to 1, as said below
- flip_out: int32 [32, 1024], P('dp'), may hold values from -1 to 1, as said below
- cotangent: bfloat16 [32, 256, 1024], P(('dp', 'seq')), may hold values from -0.75 to 0.75
Outputs:
- block_out: bfloat16 [32, 256, 1024], P(('dp', 'seq'))
- resid_grad: bfloat16 [32, 256, 1024], P(('dp', 'seq'))
- grad_mean_in: float32 [1024, 2048], P(None, 'seq')
- grad_sigma_in: float32 [1024, 2048], P(None, 'seq')
- grad_mean_out: float32 [2048, 1024], P('seq')
- grad_sigma_out: float32 [2048, 1024], P('seq')
Inputs may be any that keep to these rules, and one draw needn't show every extreme that they name: `flip_in`: each entry is -1 or +1. `flip_mid`: each entry is -1 or +1. `flip_hidden`: each entry is -1 or +1. `flip_out`: each entry is -1 or +1.
All inputs are finite; a program needn't handle non-finite values.
Results may differ from a plain program's by a relative error of at most 0.018.
Values may be sent and summed in bfloat16 or wider, within the bound.
A program may use at most 128 MiB of HBM per device.

v0:
```python
import jax
import jax.numpy as jnp
from jax import lax
from jax.sharding import PartitionSpec as P

HEADS = 16


def gelu_slope(pre):
    cdf = 0.5 * (1.0 + lax.erf(pre * 0.7071067811865476))
    pdf = jnp.exp(-0.5 * pre * pre) * 0.3989422804014327
    return cdf + pre * pdf


def contract_first(left, right):
    return lax.dot_general(
        left, right, (((0,), (0,)), ((), ())), preferred_element_type=jnp.float32
    )


def contract_last(left, right):
    return lax.dot_general(
        left, right, (((1,), (1,)), ((), ())), preferred_element_type=jnp.float32
    )


def body(
    tokens,
    queries,
    keys,
    values,
    ln_gain,
    mean_in,
    sigma_in,
    noise_in,
    mean_out,
    sigma_out,
    noise_out,
    flip_in,
    flip_mid,
    flip_hidden,
    flip_out,
    cotangent,
):
    bf = jnp.bfloat16
    f32 = jnp.float32
    own_images, patches, width = tokens.shape
    hidden_local = mean_in.shape[1]
    head_dim = width // HEADS
    scale = head_dim ** (-0.5)
    pert_in = (sigma_in.astype(f32) * noise_in.astype(f32)).astype(bf)
    pert_out = (sigma_out.astype(f32) * noise_out.astype(f32)).astype(bf)
    query_heads = queries.reshape(own_images, patches, HEADS, head_dim)
    key_heads = keys.reshape(own_images, patches, HEADS, head_dim)
    value_heads = values.reshape(own_images, patches, HEADS, head_dim)
    scores = (
        jnp.einsum("bqhe,bkhe->bhqk", query_heads, key_heads, preferred_element_type=f32) * scale
    )
    top = jnp.max(scores, axis=-1, keepdims=True)
    expd = jnp.exp(scores - top)
    total = jnp.sum(expd, axis=-1)
    accum = jnp.einsum("bhqk,bkhe->bqhe", expd.astype(bf), value_heads, preferred_element_type=f32)
    attn_out = (
        (accum / jnp.transpose(total, (0, 2, 1))[..., None])
        .reshape(own_images, patches, width)
        .astype(bf)
    )
    resid = (tokens.astype(f32) + attn_out.astype(f32)).astype(bf)
    resid_f = resid.astype(f32)
    centered = resid_f - jnp.mean(resid_f, axis=-1, keepdims=True)
    rstd = lax.rsqrt(jnp.mean(centered * centered, axis=-1, keepdims=True) + 1e-06)
    ahat = centered * rstd
    gain_f = ln_gain.astype(f32)
    normed = (ahat * gain_f).astype(bf)
    in_signs = flip_in.astype(bf)[:, None, :]
    in_signs_f = flip_in.astype(f32)[:, None, :]
    mid_signs = flip_mid.astype(bf)[:, None, :]
    mid_signs_f = flip_mid.astype(f32)[:, None, :]
    hid_signs = flip_hidden.astype(bf)[:, None, :]
    hid_signs_f = flip_hidden.astype(f32)[:, None, :]
    out_signs = flip_out.astype(bf)[:, None, :]
    out_signs_f = flip_out.astype(f32)[:, None, :]
    gathered = lax.all_gather(normed, "seq", axis=0, tiled=True)
    count = gathered.shape[0]
    signs = in_signs
    flat = gathered.reshape(-1, width)
    flat_flip = (gathered * signs).reshape(-1, width)
    plain = jnp.dot(flat, mean_in, preferred_element_type=f32).reshape(count, patches, hidden_local)
    noisy = jnp.dot(flat_flip, pert_in, preferred_element_type=f32).reshape(
        count, patches, hidden_local
    )
    pre = plain + noisy * mid_signs_f
    group_images = pre.shape[0]
    rows = group_images * patches
    hidden = jax.nn.gelu(pre, approximate=False).astype(bf)
    flipped_hidden = hidden * hid_signs
    count = lax.axis_size("seq") * own_images
    hb = hidden.reshape(-1, hidden_local)
    hfb = flipped_hidden.reshape(-1, hidden_local)
    plain = jnp.dot(hb, mean_out, preferred_element_type=f32).reshape(count, patches, width)
    noisy = jnp.dot(hfb, pert_out, preferred_element_type=f32).reshape(count, patches, width)
    mixed = lax.psum_scatter(
        (plain + noisy * out_signs_f).astype(jnp.bfloat16), "seq", scatter_dimension=0, tiled=True
    ).astype(jnp.float32)
    block_out = (resid_f + mixed).astype(bf)
    cot_all = lax.all_gather(cotangent, "seq", axis=0, tiled=True)
    cot_flat = cot_all.reshape(rows, width)
    cot_flip_flat = (cot_all * out_signs).reshape(rows, width)
    dhidden = contract_last(cot_flat, mean_out).reshape(group_images, patches, hidden_local)
    dhidden = (
        dhidden
        + contract_last(cot_flip_flat, pert_out).reshape(group_images, patches, hidden_local)
        * hid_signs_f
    )
    dpre = (dhidden * gelu_slope(pre)).astype(bf)
    dpre_flip = dpre * mid_signs
    local_mean_out = contract_first(hidden.reshape(rows, hidden_local), cot_flat)
    local_sigma_out = contract_first(
        flipped_hidden.reshape(rows, hidden_local), cot_flip_flat
    ) * noise_out.astype(f32)
    grad_mean_out, grad_sigma_out = (
        lax.psum(local_mean_out.astype(jnp.bfloat16), "dp").astype(jnp.float32),
        lax.psum(local_sigma_out.astype(jnp.bfloat16), "dp").astype(jnp.float32),
    )
    local_mean_in = contract_first(gathered.reshape(rows, width), dpre.reshape(rows, hidden_local))
    local_flip_in = contract_first(
        (gathered * in_signs).reshape(rows, width), dpre_flip.reshape(rows, hidden_local)
    )
    local_sigma_in = local_flip_in * noise_in.astype(f32)
    count = lax.axis_size("seq") * own_images
    drows = dpre.reshape(-1, hidden_local)
    dflip_rows = dpre_flip.reshape(-1, hidden_local)
    signs = in_signs_f
    plain = contract_last(drows, mean_in).reshape(count, patches, width)
    noisy = contract_last(dflip_rows, pert_in).reshape(count, patches, width)
    dnormed = lax.psum_scatter(
        (plain + noisy * signs).astype(jnp.bfloat16), "seq", scatter_dimension=0, tiled=True
    ).astype(jnp.float32)
    grad_mean_in, grad_sigma_in = (
        lax.psum(local_mean_in.astype(jnp.bfloat16), "dp").astype(jnp.float32),
        lax.psum(local_sigma_in.astype(jnp.bfloat16), "dp").astype(jnp.float32),
    )
    scaled = dnormed * gain_f
    back = rstd * (
        scaled
        - jnp.mean(scaled, axis=-1, keepdims=True)
        - ahat * jnp.mean(scaled * ahat, axis=-1, keepdims=True)
    )
    resid_grad = (cotangent.astype(f32) + back).astype(bf)
    return (block_out, resid_grad, grad_mean_in, grad_sigma_in, grad_mean_out, grad_sigma_out)


def solution(mesh):
    return jax.shard_map(
        body,
        mesh=mesh,
        in_specs=(
            P(("dp", "seq"), None, None),
            P(("dp", "seq"), None, None),
            P(("dp", "seq"), None, None),
            P(("dp", "seq"), None, None),
            P(),
            P(None, "seq"),
            P(None, "seq"),
            P(None, "seq"),
            P("seq", None),
            P("seq", None),
            P("seq", None),
            P("dp", None),
            P("dp", "seq"),
            P("dp", "seq"),
            P("dp", None),
            P(("dp", "seq"), None, None),
        ),
        out_specs=(
            P(("dp", "seq"), None, None),
            P(("dp", "seq"), None, None),
            P(None, "seq"),
            P(None, "seq"),
            P("seq", None),
            P("seq", None),
        ),
        check_vma=False,
    )
```

profile of v0, /device:TPU:0, one launch (start us, length us, event | category | flops | bytes accessed | tf_op | source)
XLA Modules:
  0.0 289.0 jit_solution(1723222755347720097)
XLA Ops:
  7.2 0.0 copy-start
  7.2 0.0 all-gather.3.cloned.1.call-start
  7.2 1.4 copy.42
  8.6 1.2 copy.40
  9.9 0.2 copy.41
  10.1 0.8 multiply_reduce_fusion
  10.8 0.7 fusion
  11.6 0.9 divide_convert_fusion
  12.5 0.1 bitcast_convert_fusion.2
  12.6 1.3 copy.44
  13.9 1.5 convert_reduce_fusion
  15.5 0.3 fusion.51
  15.8 1.1 fusion.45
  16.9 0.0 all-gather.3.cloned.1.call-update
  16.9 0.0 all-gather.5.cloned.1.call-start
  16.9 0.7 all-gather.5.cloned.1.call-update
  17.6 0.2 all-reduce.5.cloned.1.call-start
  18.0 37.0 %all-gather.3.cloned.1.call-done = bf16[4,256,1024]{2,1,0:T(8,128)(2,1)} async-done(((bf16[1,256,1024]{2,1,0:T(8,128)(2,1)}), bf16[4,256,1024]{2,1,0:T(8,128)(2,1)}) %all-gather.3.cloned.1.call-update) | async-done | bytes 2097168 | tf_op jit(solution)/shard_map/all_gather | solution.py:83
  55.0 3.3 %fusion.31 = f32[4,256,512]{2,1,0:T(8,128)S(1)} fusion(bf16[4,256,1024]{2,1,0:T(8,128)(2,1)} %all-gather.3.cloned.1.call-done, bf16[4,1024]{1,0:T(4,128)(2,1)S(1)} %get-tuple-element.19, bf16[1024,512]{1,0:T(8,128)(2,1)S(1)} %copy-done.7, bf16[1024,512]{1,0:T(8,128)(2,1)} %param.22), kind=kOutput, calls=%fused_computation.55 | convolution fusion | flops 1076887552 | bytes 6299648 | tf_op jit(solution)/shard_map/dot_general | solution.py:89
  58.3 1.9 fusion.77
  60.2 1.3 copy-done.4
  61.5 4.7 %fusion.8 = bf16[4,256,512]{2,1,0:T(8,128)(2,1)S(1)} fusion(f32[4,256,512]{2,1,0:T(8,128)S(1)} %get-tuple-element.28, u8[256,512]{1,0:T(8,128)(4,1)S(1)} %get-tuple-element.7, u8[256,512]{1,0:T(8,128)(4,1)S(1)} %get-tuple-element.6), kind=kLoop, calls=%fused_computation.18 | loop fusion | flops 36700160 | bytes 3407872 | tf_op jit(solution)/shard_map/convert_element_type | solution.py:95
  66.2 25.8 %all-gather.5.cloned.1.call-done = bf16[4,256,1024]{2,1,0:T(8,128)(2,1)} async-done(((bf16[1,256,1024]{2,1,0:T(8,128)(2,1)}), bf16[4,256,1024]{2,1,0:T(8,128)(2,1)}) %all-gather.5.cloned.1.call-update) | async-done | bytes 2097168 | tf_op jit(solution)/shard_map/all_gather | solution.py:106
  92.0 3.6 %fusion.27 = f32[4,256,512]{2,1,0:T(8,128)S(1)} fusion(bf16[4,256,1024]{2,1,0:T(8,128)(2,1)} %all-gather.5.cloned.1.call-done, bf16[4,1024]{1,0:T(4,128)(2,1)S(1)} %get-tuple-element.20, bf16[512,1024]{1,0:T(8,128)(2,1)} %param.26, bf16[512,1024]{1,0:T(8,128)(2,1)} %param.25), kind=kOutput, calls=%fused_computation.51 | convolution fusion | flops 1076887552 | bytes 6299648 | tf_op jit(solution)/shard_map/dot_general | solution.py:22
  95.7 0.1 copy-done.17
  95.8 2.0 fusion.14
  97.8 2.3 bitcast_convert_fusion.1
  100.1 2.3 fusion.3
  102.4 2.3 bitcast_convert_fusion
  104.6 2.4 fusion.5
  107.0 0.0 all-reduce.5.cloned.1.call-update
  107.0 0.3 reduce-scatter.9.cloned.1.call-start
  107.3 2.7 fusion.58
  110.0 2.6 add_convert_fusion
  112.6 0.0 reduce-scatter.9.cloned.1.call-update
  112.7 0.0 reduce-scatter.7.cloned.1.call-start
  112.7 2.6 fusion.56
  115.4 2.6 add_convert_fusion.1
  118.0 0.0 reduce-scatter.7.cloned.1.call-update
  118.0 85.7 %all-reduce.5.cloned.1.call-done = (bf16[1024,512]{1,0:T(8,128)(2,1)}, bf16[1024,512]{1,0:T(8,128)(2,1)}, bf16[512,1024]{1,0:T(8,128)(2,1)}, bf16[512,1024]{1,0:T(8,128)(2,1)}) async-done(((bf16[1024,512]{1,0:T(8,128)(2,1)}, bf16[1024,512]{1,0:T(8,128)(2,1)}, bf16[512,1024]{1,0:T(8,128)(2,1)}, bf16[512,1024]{1,0:T(8,128)(2,1)}), (bf16[1024,512]{1,0:T(8,128)(2,1)}, bf16[1024,512]{1,0:T(8,128)(2,1)}, ...) | async-done | bytes 4194320 | tf_op jit(solution)/shard_map/psum | solution.py:140
  203.7 2.9 %convert_element_type.173 = f32[1024,512]{1,0:T(8,128)} convert(bf16[1024,512]{1,0:T(8,128)(2,1)} %get-tuple-element.10) | non-fusion elementwise | flops 524288 | bytes 3145728 | tf_op jit(solution)/shard_map/convert_element_type | solution.py:140
  206.7 1.6 convert_element_type.175
  208.3 1.6 convert_element_type.177
  209.8 1.6 convert_element_type.179
  211.4 30.4 %reduce-scatter.9.cloned.1.call-done = bf16[1,256,1024]{2,1,0:T(8,128)(2,1)} async-done(((bf16[4,256,1024]{2,1,0:T(8,128)(2,1)}), bf16[1,256,1024]{2,1,0:T(8,128)(2,1)}) %reduce-scatter.9.cloned.1.call-update) | async-done | bytes 524304
  241.8 1.4 fusion.61
  243.2 36.6 %reduce-scatter.7.cloned.1.call-done = bf16[1,256,1024]{2,1,0:T(8,128)(2,1)} async-done(((bf16[4,256,1024]{2,1,0:T(8,128)(2,1)}), bf16[1,256,1024]{2,1,0:T(8,128)(2,1)}) %reduce-scatter.7.cloned.1.call-update) | async-done | bytes 524304
  279.8 2.6 fusion.50
  (59 shorter events, 0.2 us)
Async XLA Ops:
  7.2 51.1 %copy-start = (bf16[1024,512]{1,0:T(8,128)(2,1)S(1)}, bf16[1024,512]{1,0:T(8,128)(2,1)}, u32[]{:S(2)}) copy-start(bf16[1024,512]{1,0:T(8,128)(2,1)} %param.21) | copy-start | bytes 3145732
  7.2 2.7 copy-start.18
  7.2 47.8 %all-gather.3.cloned.1.call-start = ((), (), s32[]{:S(2)}) async-start(), calls=%async_computation.2 | async-start | bytes 2621440 | tf_op jit(solution)/shard_map/all_gather | solution.py:83
  12.4 1.4 copy-start.24
  12.4 1.4 copy-start.19
  13.9 4.0 %copy-start.22 = (s32[4,512]{1,0:T(4,128)S(1)}, s32[4,512]{1,0:T(4,128)}, u32[]{:S(2)}) copy-start(s32[4,512]{1,0:T(4,128)} %param.28) | copy-start | bytes 24580
  13.9 4.0 %copy-start.23 = (s32[4,512]{1,0:T(4,128)S(1)}, s32[4,512]{1,0:T(4,128)}, u32[]{:S(2)}) copy-start(s32[4,512]{1,0:T(4,128)} %param.29) | copy-start | bytes 24580
  13.9 4.0 %copy-start.20 = (s32[4,1024]{1,0:T(4,128)S(1)}, s32[4,1024]{1,0:T(4,128)}, u32[]{:S(2)}) copy-start(s32[4,1024]{1,0:T(4,128)} %param.27) | copy-start | bytes 49156
  13.9 4.0 %copy-start.21 = (s32[4,1024]{1,0:T(4,128)S(1)}, s32[4,1024]{1,0:T(4,128)}, u32[]{:S(2)}) copy-start(s32[4,1024]{1,0:T(4,128)} %param.30) | copy-start | bytes 49156
  13.9 41.0 %copy-start.7 = (bf16[1024,512]{1,0:T(8,128)(2,1)S(1)}, bf16[1024,512]{1,0:T(8,128)(2,1)}, u32[]{:S(2)}) copy-start(bf16[1024,512]{1,0:T(8,128)(2,1)} %param.23) | copy-start | bytes 3145732
  16.9 75.1 %all-gather.5.cloned.1.call-start = ((), (), s32[]{:S(2)}) async-start(), calls=%async_computation.3 | async-start | bytes 2621440 | tf_op jit(solution)/shard_map/all_gather | solution.py:106
  17.6 186.1 %all-reduce.5.cloned.1.call-start = ((), (), s32[]{:S(2)}) async-start(), calls=%async_computation.6 | async-start | bytes 8388608 | tf_op jit(solution)/shard_map/psum | solution.py:140
  55.0 3.3 %copy-start.25 = (bf16[4,256,1024]{2,1,0:T(8,128)(2,1)S(1)}, bf16[4,256,1024]{2,1,0:T(8,128)(2,1)}, u32[]{:S(2)}) copy-start(bf16[4,256,1024]{2,1,0:T(8,128)(2,1)} %all-gather.3.cloned.1.call-done) | copy-start | bytes 6291460
  60.2 1.3 copy-start.4
  92.0 3.6 %copy-start.3 = (bf16[4,256,1024]{2,1,0:T(8,128)(2,1)S(1)}, bf16[4,256,1024]{2,1,0:T(8,128)(2,1)}, u32[]{:S(2)}) copy-start(bf16[4,256,1024]{2,1,0:T(8,128)(2,1)} %all-gather.5.cloned.1.call-done) | copy-start | bytes 6291460
  92.0 3.6 %copy-start.5 = (f32[4,256,512]{2,1,0:T(8,128)S(1)}, f32[4,256,512]{2,1,0:T(8,128)}, u32[]{:S(2)}) copy-start(f32[4,256,512]{2,1,0:T(8,128)} %copy-done.4) | copy-start | bytes 6291460
  92.0 3.7 %copy-start.17 = (bf16[512,1024]{1,0:T(8,128)(2,1)S(1)}, bf16[512,1024]{1,0:T(8,128)(2,1)}, u32[]{:S(2)}) copy-start(bf16[512,1024]{1,0:T(8,128)(2,1)} %param.24) | copy-start | bytes 3145732
  95.8 2.1 copy-start.26
  97.8 2.3 copy-start.1
  97.8 2.3 copy-start.8
  102.4 2.3 copy-start.11
  107.0 134.8 %reduce-scatter.9.cloned.1.call-start = ((), (), s32[]{:S(2)}) async-start(), calls=%async_computation.5 | async-start | bytes 2621440
  107.3 2.7 copy-start.2
  107.3 2.7 copy-start.9
  107.3 2.7 copy-start.10
  112.7 167.2 %reduce-scatter.7.cloned.1.call-start = ((), (), s32[]{:S(2)}) async-start(), calls=%async_computation.4 | async-start | bytes 2621440
  112.7 2.7 copy-start.12
  112.7 2.7 copy-start.13
  203.7 2.9 %copy-start.16 = (bf16[1024,512]{1,0:T(8,128)(2,1)S(1)}, bf16[1024,512]{1,0:T(8,128)(2,1)}, u32[]{:S(2)}) copy-start(bf16[1024,512]{1,0:T(8,128)(2,1)} %get-tuple-element.11) | copy-start | bytes 3145732
  206.6 1.6 copy-start.15
  208.3 1.6 copy-start.14
  209.8 70.0 %copy-start.6 = (bf16[1,256,1024]{2,1,0:T(8,128)(2,1)S(1)}, bf16[1,256,1024]{2,1,0:T(8,128)(2,1)}, u32[]{:S(2)}) copy-start(bf16[1,256,1024]{2,1,0:T(8,128)(2,1)} %param.31) | copy-start | bytes 1572868
Sparse Core Ops, SparseCore 0:
  17.0 37.8 all-gather.2
  56.8 35.1 all-gather.4
  107.1 96.5 all-reduce.4
  206.5 35.2 reduce-scatter.8
  244.6 35.1 reduce-scatter.6
where the time goes:
time: 289 us
  waiting for transfers between devices  216 us (75%)
  matrix products  32.2 us (11%)
  other arithmetic  20.2 us (7%)
  between operations  14.2 us (5%)
  local copies, waits for them, and re-layouts  5.66 us (2%)
    psum x1, waiting for transfers between devices, body(): lax.psum(local_mean_in.astype(jnp.bfloat16), 'dp').astype(jnp.float32)  85.7 us
    unnamed x7, waiting for transfers between devices  67.8 us
    all_gather x1, waiting for transfers between devices, body(): gathered = lax.all_gather(normed, 'seq', axis=0, tiled=True)  37 us
    all_gather x1, waiting for transfers between devices, body(): cot_all = lax.all_gather(cotangent, 'seq', axis=0, tiled=True)  25.8 us
    dot_general x4, matrix products, contract_last(): lax.dot_general(left, right, (((1,), (1,)), ((), ())), preferred_element_...  11 us
    dot_general x4, matrix products, contract_first(): lax.dot_general(left, right, (((0,), (0,)), ((), ())), preferred_element_...  9.14 us
  transfers between devices with their start and end apart: 5, of which 5 were waited for; matrix products, arithmetic and copies ran while one was open for 10% of the time, Pallas kernels for 0%

commit v1 on v0

--- a/solution.py
+++ b/solution.py
@@ -1,9 +1,18 @@
+import functools
 import jax
 import jax.numpy as jnp
 from jax import lax
 from jax.sharding import PartitionSpec as P
 
 HEADS = 16
+
+
+def detail_surface_over_axis(vals, axis_name):
+    mid_arr = jnp.sum(lax.all_gather(vals, axis_name), 0)
+    return mid_arr
+
+
+samples_handle = functools.partial(detail_surface_over_axis, axis_name="dp")
 
 
 def gelu_slope(pre):
@@ -137,7 +146,7 @@
         (plain + noisy * signs).astype(jnp.bfloat16), "seq", scatter_dimension=0, tiled=True
     ).astype(jnp.float32)
     grad_mean_in, grad_sigma_in = (
-        lax.psum(local_mean_in.astype(jnp.bfloat16), "dp").astype(jnp.float32),
+        samples_handle(local_mean_in.astype(jnp.bfloat16)).astype(jnp.float32),
         lax.psum(local_sigma_in.astype(jnp.bfloat16), "dp").astype(jnp.float32),
     )
     scaled = dnormed * gain_f

time: 289 us -> 356 us (1.23)
  waiting for transfers between devices: 216 us -> 274 us
  other arithmetic: 20.2 us -> 25.4 us
    all_gather x0 -> x1, waiting for transfers between devices: none -> 80.9 us  [detail_surface_over_axis(): mid_arr = jnp.sum(lax.all_gather(vals, axis_name), 0)]
    psum x1, waiting for transfers between devices: 85.7 us -> 60.8 us  [body(): lax.psum(local_sigma_in.astype(jnp.bfloat16), 'dp').astype(jnp.float32)]
    reduce_sum x0 -> x1, other arithmetic: none -> 5.24 us  [detail_surface_over_axis(): mid_arr = jnp.sum(lax.all_gather(vals, axis_name), 0)]
    unnamed x7 -> x8, waiting for transfers between devices: 67.8 us -> 70 us
  transfers between devices with their start and end apart: 5 -> 6, of which waited for: 5 -> 6; matrix products, arithmetic and copies ran while one was open for 10% -> 10% of each run, Pallas kernels for 0% -> 0%
where the time goes in v1:
time: 356 us
  waiting for transfers between devices  274 us (77%)
  matrix products  33.2 us (9%)
  other arithmetic  25.4 us (7%)
  between operations  14.5 us (4%)
  local copies, waits for them, and re-layouts  7.7 us (2%)
    all_gather x1, waiting for transfers between devices, detail_surface_over_axis(): mid_arr = jnp.sum(lax.all_gather(vals, axis_name), 0)  80.9 us
    unnamed x8, waiting for transfers between devices  70 us
    psum x1, waiting for transfers between devices, body(): lax.psum(local_sigma_in.astype(jnp.bfloat16), 'dp').astype(jnp.float32)  60.8 us
    all_gather x1, waiting for transfers between devices, body(): gathered = lax.all_gather(normed, 'seq', axis=0, tiled=True)  37 us
    all_gather x1, waiting for transfers between devices, body(): cot_all = lax.all_gather(cotangent, 'seq', axis=0, tiled=True)  25.8 us
    dot_general x4, matrix products, contract_first(): lax.dot_general(left, right, (((0,), (0,)), ((), ())), preferred_element_...  12.4 us
    dot_general x4, matrix products, contract_last(): lax.dot_general(left, right, (((1,), (1,)), ((), ())), preferred_element_...  8.64 us
  transfers between devices with their start and end apart: 6, of which 6 were waited for; matrix products, arithmetic and copies ran while one was open for 10% of the time, Pallas kernels for 0%

profile of v1, /device:TPU:0, one launch (start us, length us, event | category | flops | bytes accessed | tf_op | source)
XLA Modules:
  0.0 355.9 jit_solution(1733378226351158116)
XLA Ops:
  7.2 0.0 all-gather.5.cloned.1.call-start
  7.2 1.4 copy.42
  8.6 1.2 copy.40
  9.9 0.2 copy.41
  10.1 0.8 multiply_reduce_fusion
  10.8 0.7 fusion
  11.6 0.9 divide_convert_fusion
  12.5 0.1 bitcast_convert_fusion.2
  12.6 1.3 copy.44
  14.0 1.5 convert_reduce_fusion
  15.5 0.3 fusion.51
  15.8 1.1 fusion.45
  16.9 0.0 all-gather.5.cloned.1.call-update
  16.9 0.0 all-gather.7.cloned.1.call-start
  16.9 0.7 all-gather.7.cloned.1.call-update
  17.7 0.2 all-reduce.5.cloned.1.call-start
  18.0 37.0 %all-gather.5.cloned.1.call-done = bf16[4,256,1024]{2,1,0:T(8,128)(2,1)} async-done(((bf16[1,256,1024]{2,1,0:T(8,128)(2,1)}), bf16[4,256,1024]{2,1,0:T(8,128)(2,1)}) %all-gather.5.cloned.1.call-update) | async-done | bytes 2097168 | tf_op jit(solution)/shard_map/all_gather | solution.py:92
  55.0 3.3 fusion.31
  58.3 1.9 fusion.77
  60.2 1.3 copy-done.5
  61.5 4.7 %fusion.8 = bf16[4,256,512]{2,1,0:T(8,128)(2,1)S(1)} fusion(f32[4,256,512]{2,1,0:T(8,128)S(1)} %get-tuple-element.27, u8[256,512]{1,0:T(8,128)(4,1)S(1)} %get-tuple-element.7, u8[256,512]{1,0:T(8,128)(4,1)S(1)} %get-tuple-element.6), kind=kLoop, calls=%fused_computation.18 | loop fusion | flops 36700160 | bytes 3407872 | tf_op jit(solution)/shard_map/convert_element_type | solution.py:104
  66.2 25.8 %all-gather.7.cloned.1.call-done = bf16[4,256,1024]{2,1,0:T(8,128)(2,1)} async-done(((bf16[1,256,1024]{2,1,0:T(8,128)(2,1)}), bf16[4,256,1024]{2,1,0:T(8,128)(2,1)}) %all-gather.7.cloned.1.call-update) | async-done | bytes 2097168 | tf_op jit(solution)/shard_map/all_gather | solution.py:115
  92.0 4.0 %bitcast_convert_fusion = bf16[512,1024]{1,0:T(8,128)(2,1)} fusion(bf16[4,256,512]{2,1,0:T(8,128)(2,1)S(1)} %fusion.8, bf16[4,256,1024]{2,1,0:T(8,128)(2,1)} %all-gather.7.cloned.1.call-done), kind=kOutput, calls=%fused_computation.31 | convolution fusion | flops 1074266112 | bytes 4194304 | tf_op jit(solution)/shard_map/dot_general | solution.py:25
  96.0 1.3 fusion.27
  97.3 2.3 fusion.5
  99.6 2.1 fusion.14
  101.7 1.0 copy-done.1
  102.7 2.3 fusion.3
  105.0 0.3 reduce-scatter.9.cloned.1.call-start
  105.3 2.7 fusion.58
  108.0 2.6 add_convert_fusion
  110.6 0.0 reduce-scatter.7.cloned.1.call-start
  110.7 2.6 fusion.56
  113.3 2.7 add_convert_fusion.1
  116.1 0.0 all-gather.9.cloned.1.call-start
  116.1 1.2 copy-done.3
  117.3 3.9 %bitcast_convert_fusion.1 = bf16[1024,512]{1,0:T(8,128)(2,1)} fusion(bf16[4,256,1024]{2,1,0:T(8,128)(2,1)} %all-gather.5.cloned.1.call-done, bf16[4,256,512]{2,1,0:T(8,128)(2,1)S(1)} %copy-done.3), kind=kOutput, calls=%fused_computation.32 | convolution fusion | flops 1074266112 | bytes 4194304 | tf_op jit(solution)/shard_map/dot_general | solution.py:25
  121.2 60.8 %all-reduce.5.cloned.1.call-done = (bf16[1024,512]{1,0:T(8,128)(2,1)}, bf16[512,1024]{1,0:T(8,128)(2,1)}, bf16[512,1024]{1,0:T(8,128)(2,1)}) async-done(((bf16[1024,512]{1,0:T(8,128)(2,1)}, bf16[512,1024]{1,0:T(8,128)(2,1)}, bf16[512,1024]{1,0:T(8,128)(2,1)}), (bf16[1024,512]{1,0:T(8,128)(2,1)}, bf16[512,1024]{1,0:T(8,128)(2,1)}, bf16[512,1024]{1,0:T(8,128)(2,1)})) %all-reduce.5.cloned.1.call-update) | async-done | bytes 3145744 | tf_op jit(solution)/shard_map/psum | solution.py:150
  182.0 2.9 convert_element_type.177
  184.9 1.6 convert_element_type.179
  186.5 1.6 convert_element_type.181
  188.0 32.5 %reduce-scatter.9.cloned.1.call-done = bf16[1,256,1024]{2,1,0:T(8,128)(2,1)} async-done(((bf16[4,256,1024]{2,1,0:T(8,128)(2,1)}), bf16[1,256,1024]{2,1,0:T(8,128)(2,1)}) %reduce-scatter.9.cloned.1.call-update) | async-done | bytes 524304
  220.6 1.4 fusion.61
  222.0 36.6 %reduce-scatter.7.cloned.1.call-done = bf16[1,256,1024]{2,1,0:T(8,128)(2,1)} async-done(((bf16[4,256,1024]{2,1,0:T(8,128)(2,1)}), bf16[1,256,1024]{2,1,0:T(8,128)(2,1)}) %reduce-scatter.7.cloned.1.call-update) | async-done | bytes 524304
  258.6 2.6 fusion.50
  261.2 80.9 %all-gather.9.cloned.1.call-done = bf16[8192,512]{1,0:T(8,128)(2,1)} async-done(((bf16[1024,512]{1,0:T(8,128)(2,1)}), bf16[8192,512]{1,0:T(8,128)(2,1)}) %all-gather.9.cloned.1.call-update) | async-done | bytes 8388624 | tf_op jit(solution)/shard_map/all_gather | solution.py:11
  342.2 5.2 %reduce_sum.65 = bf16[1024,512]{1,0:T(8,128)(2,1)S(1)} reduce(bf16[8,1024,512]{2,1,0:T(8,128)(2,1)} %bitcast.60, bf16[]{:T(256)} %constant.78.clone.1), dimensions={0}, to_apply=%region_8.0 | reduce | flops 3670016 | bytes 9437186 | tf_op jit(solution)/shard_map/reduce_sum | solution.py:11
  347.4 1.6 convert_element_type.175
  (65 shorter events, 0.3 us)
Async XLA Ops:
  7.2 51.1 %copy-start = (bf16[1024,512]{1,0:T(8,128)(2,1)S(1)}, bf16[1024,512]{1,0:T(8,128)(2,1)}, u32[]{:S(2)}) copy-start(bf16[1024,512]{1,0:T(8,128)(2,1)} %param.21) | copy-start | bytes 3145732
  7.2 2.7 copy-start.19
  7.2 47.8 %all-gather.5.cloned.1.call-start = ((), (), s32[]{:S(2)}) async-start(), calls=%async_computation.2 | async-start | bytes 2621440 | tf_op jit(solution)/shard_map/all_gather | solution.py:92
  12.4 1.4 copy-start.25
  12.5 1.4 copy-start.20
  13.9 4.0 %copy-start.23 = (s32[4,512]{1,0:T(4,128)S(1)}, s32[4,512]{1,0:T(4,128)}, u32[]{:S(2)}) copy-start(s32[4,512]{1,0:T(4,128)} %param.28) | copy-start | bytes 24580
  13.9 4.0 %copy-start.24 = (s32[4,512]{1,0:T(4,128)S(1)}, s32[4,512]{1,0:T(4,128)}, u32[]{:S(2)}) copy-start(s32[4,512]{1,0:T(4,128)} %param.29) | copy-start | bytes 24580
  13.9 4.0 %copy-start.21 = (s32[4,1024]{1,0:T(4,128)S(1)}, s32[4,1024]{1,0:T(4,128)}, u32[]{:S(2)}) copy-start(s32[4,1024]{1,0:T(4,128)} %param.27) | copy-start | bytes 49156
  13.9 4.0 %copy-start.22 = (s32[4,1024]{1,0:T(4,128)S(1)}, s32[4,1024]{1,0:T(4,128)}, u32[]{:S(2)}) copy-start(s32[4,1024]{1,0:T(4,128)} %param.30) | copy-start | bytes 49156
  13.9 41.0 %copy-start.8 = (bf16[1024,512]{1,0:T(8,128)(2,1)S(1)}, bf16[1024,512]{1,0:T(8,128)(2,1)}, u32[]{:S(2)}) copy-start(bf16[1024,512]{1,0:T(8,128)(2,1)} %param.23) | copy-start | bytes 3145732
  16.9 75.1 %all-gather.7.cloned.1.call-start = ((), (), s32[]{:S(2)}) async-start(), calls=%async_computation.3 | async-start | bytes 2621440 | tf_op jit(solution)/shard_map/all_gather | solution.py:115
  17.7 164.3 %all-reduce.5.cloned.1.call-start = ((), (), s32[]{:S(2)}) async-start(), calls=%async_computation.7 | async-start | bytes 6291456 | tf_op jit(solution)/shard_map/psum | solution.py:150
  55.0 3.3 copy-start.26
  60.2 1.3 copy-start.5
  92.0 4.0 %copy-start.4 = (bf16[4,256,1024]{2,1,0:T(8,128)(2,1)S(1)}, bf16[4,256,1024]{2,1,0:T(8,128)(2,1)}, u32[]{:S(2)}) copy-start(bf16[4,256,1024]{2,1,0:T(8,128)(2,1)} %all-gather.7.cloned.1.call-done) | copy-start | bytes 6291460
  92.0 4.0 %copy-start.12 = (bf16[512,1024]{1,0:T(8,128)(2,1)S(1)}, bf16[512,1024]{1,0:T(8,128)(2,1)}, u32[]{:S(2)}) copy-start(bf16[512,1024]{1,0:T(8,128)(2,1)} %param.26) | copy-start | bytes 3145732
  92.0 4.0 %copy-start.14 = (bf16[512,1024]{1,0:T(8,128)(2,1)S(1)}, bf16[512,1024]{1,0:T(8,128)(2,1)}, u32[]{:S(2)}) copy-start(bf16[512,1024]{1,0:T(8,128)(2,1)} %param.25) | copy-start | bytes 3145732
  97.3 2.3 copy-start.6
  97.3 2.3 copy-start.18
  99.6 3.1 copy-start.9
  99.6 3.1 copy-start.27
  101.7 1.0 copy-start.1
  105.0 115.6 %reduce-scatter.9.cloned.1.call-start = ((), (), s32[]{:S(2)}) async-start(), calls=%async_computation.6 | async-start | bytes 2621440
  105.2 2.7 copy-start.2
  105.3 2.7 copy-start.10
  105.3 2.7 copy-start.11
  110.6 148.0 %reduce-scatter.7.cloned.1.call-start = ((), (), s32[]{:S(2)}) async-start(), calls=%async_computation.5 | async-start | bytes 2621440
  110.7 2.7 copy-start.13
  110.7 2.7 copy-start.15
  116.0 1.2 copy-start.3
  116.1 226.1 %all-gather.9.cloned.1.call-start = ((), (), s32[]{:S(2)}) async-start(), calls=%async_computation.4 | async-start | bytes 9437184 | tf_op jit(solution)/shard_map/all_gather | solution.py:11
  182.0 2.9 copy-start.17
  184.9 1.6 copy-start.16
  186.5 72.2 %copy-start.7 = (bf16[1,256,1024]{2,1,0:T(8,128)(2,1)S(1)}, bf16[1,256,1024]{2,1,0:T(8,128)(2,1)}, u32[]{:S(2)}) copy-start(bf16[1,256,1024]{2,1,0:T(8,128)(2,1)} %param.31) | copy-start | bytes 1572868
Sparse Core Ops, SparseCore 0:
  17.0 37.8 all-gather.4
  56.8 35.1 all-gather.6
  105.1 76.8 all-reduce.4
  185.4 35.1 reduce-scatter.8
  223.4 35.1 reduce-scatter.6
  260.1 82.0 all-gather.8
